TPU v7x, 256 devices: a whole 4x4x8 slice. The times are simulated.
256 devices in a mesh: grp: 4 (over y), dev: 64 (over z, x, core).
Axes of the slice: x: 4, y: 4, z: 8, core: 2. Of those that a mesh axis runs over, the one named last changes fastest.
Arguments:
- pool_latent: bfloat16 [512, 256, 512], P(('grp', 'dev')), may hold values from -6 to 6
- pool_rope: bfloat16 [512, 64, 256], P(('grp', 'dev')), may hold values from -6 to 6
- q_nope: bfloat16 [1024, 16384], P(None, 'dev'), may hold values from -6 to 6
- q_rope: bfloat16 [1024, 8192], P(None, 'dev'), may hold values from -9 to 9
- w_uk: bfloat16 [512, 16384], P(None, 'dev'), may hold values from -0.25 to 0.25
- w_uv: bfloat16 [512, 16384], P(None, 'dev'), may hold values from -0.25 to 0.25
- w_o: bfloat16 [16384, 7168], P('dev'), may hold values from -0.046875 to 0.046875
- block_table: int32 [64, 8], replicated, may hold values from 0 to 511, as said below
- lengths: int32 [64], replicated, may hold values from 2 to 2048, as said below
- preempted: int32 [32], replicated, may hold values from 0 to 63, as said below
- assignment: int32 [32], replicated, may hold values from 0 to 3, as said below
Outputs:
- mixed: bfloat16 [1024, 7168], P('grp', 'dev')
Inputs may be any that keep to these rules, and one draw needn't show every extreme that they name: `preempted`: distinct slots. `assignment`: each group receives exactly 8 requests. `block_table`: every page number 0 to 511 appears exactly once in the table; page p lies on the device with index p // 2 along grp+dev, at position p % 2 there. For every group and every index along dev, exactly 1 of the pages listed for the slots of that group's requests lie on devices with that index along dev. `lengths`: in every draw all requests of one group hold more than (7) * 256 tokens.
All inputs are finite; a program needn't handle non-finite values.
Results may differ from a plain program's by a relative error of at most 0.015.
Values may be sent and summed in bfloat16 or wider, within the bound.
No kernel may reach another device: no remote copies, remote signals or barrier semaphores. Data moves between devices by JAX's collectives and lax.ppermute only.
A program may use at most 128 MiB of HBM per device.

v0:
```python
import math
import jax
import jax.numpy as jnp
from jax import lax
from jax.sharding import Mesh
from jax.sharding import PartitionSpec as P

DR = 64
DN = 128
DV = 128
DEV = ("dev_0", "dev_1", "dev_2")
GRP_DEV = ("grp", "dev_0", "dev_1", "dev_2")
NEG = -1e30


def sent_together(arrays, axis, split_dim, concat_dim, along):
    widths = [math.prod(a.shape[along:]) for a in arrays]
    both = jnp.concatenate(
        [a.reshape(*a.shape[:along], w) for a, w in zip(arrays, widths)], axis=along
    )
    filled = lax.all_to_all(both, axis, split_axis=split_dim, concat_axis=concat_dim, tiled=True)
    tiles = jnp.split(filled, [sum(widths[:k]) for k in range(1, len(widths))], axis=along)
    return tuple(
        (b.reshape(*filled.shape[:along], *a.shape[along:]) for a, b in zip(arrays, tiles))
    )


def summed_rows(so_far, axes):
    for axis in axes:
        so_far = lax.psum_scatter(so_far, axis, scatter_dimension=0, tiled=True)
    return so_far


def place_values(targets, values, length, dtype):
    return jnp.zeros((length + 1,), dtype).at[targets].set(values)[:length]


def local(
    pool_latent,
    pool_rope,
    q_nope,
    q_rope,
    w_uk,
    w_uv,
    w_o,
    block_table,
    lengths,
    preempted,
    assignment,
):
    groups = lax.axis_size("grp")
    columns = lax.axis_size(DEV)
    group = lax.axis_index("grp")
    column = lax.axis_index(DEV)
    pages_dev = pool_latent.shape[0]
    block = pool_latent.shape[1]
    latent_width = pool_latent.shape[2]
    rope_width = pool_rope.shape[1]
    requests = preempted.shape[0]
    blocks = block_table.shape[1]
    per_group = requests // groups
    group_pages = per_group * blocks
    per_column = group_pages // columns
    query_rows = q_nope.shape[0] // requests
    heads_dev = q_rope.shape[1] // rope_width
    scale = 1.0 / math.sqrt(DN + DR)
    slot_pages = block_table[preempted]
    slot_len = lengths[preempted]
    req_ids = jnp.arange(requests, dtype=jnp.int32)
    earlier = (assignment[:, None] == assignment[None, :]) & (req_ids[None, :] < req_ids[:, None])
    rank = jnp.sum(earlier.astype(jnp.int32), axis=1)
    entries = requests * blocks
    entry_ids = jnp.arange(entries, dtype=jnp.int32)
    entry_page = slot_pages.reshape(entries)
    entry_req = entry_ids // blocks
    entry_block = entry_ids % blocks
    entry_group = assignment[entry_req]
    holder = entry_page // pages_dev
    entry_row = holder // columns
    entry_col = holder % columns
    entry_local = entry_page % pages_dev
    entry_key = entry_col * groups + entry_group
    before = (entry_key[:, None] == entry_key[None, :]) & (entry_ids[None, :] < entry_ids[:, None])
    entry_slot = jnp.sum(before.astype(jnp.int32), axis=1)
    entry_pos = entry_col * per_column + entry_slot
    entry_valid = jnp.clip(slot_len[entry_req] - entry_block * block, 0, block)
    outgoing = groups * per_column
    sending = (entry_row == group) & (entry_col == column)
    send_target = jnp.where(sending, entry_group * per_column + entry_slot, outgoing)
    send_index = place_values(send_target, entry_local, outgoing, jnp.int32)
    send_live = place_values(send_target, jnp.ones((entries,), jnp.bool_), outgoing, jnp.bool_)
    zero = jnp.zeros((), pool_latent.dtype)
    out_latent = jnp.where(send_live[:, None, None], pool_latent[send_index], zero)
    out_rope = jnp.where(send_live[:, None, None], pool_rope[send_index], zero)
    got_latent, got_rope = sent_together((out_latent, out_rope), "grp", 0, 0, 1)
    mine = (entry_group == group) & (entry_col == column)
    source = place_values(jnp.where(mine, entry_slot, per_column), entry_row, per_column, jnp.int32)
    pick = source * per_column + jnp.arange(per_column, dtype=jnp.int32)
    own_latent = got_latent[pick]
    own_rope = got_rope[pick]
    in_group = entry_group == group
    pos_target = jnp.where(in_group, entry_pos, group_pages)
    page_req = place_values(pos_target, rank[entry_req], group_pages, jnp.int32)
    page_valid = place_values(pos_target, entry_valid, group_pages, jnp.int32)
    members = place_values(
        jnp.where(assignment == group, rank, per_group), req_ids, per_group, jnp.int32
    )
    rows = (
        members[:, None] * query_rows + jnp.arange(query_rows, dtype=jnp.int32)[None, :]
    ).reshape(-1)
    query_lo = q_nope[rows].reshape(per_group * query_rows, heads_dev, DN)
    query_hi = q_rope[rows].reshape(per_group, query_rows, heads_dev, rope_width)
    w_key = w_uk.reshape(latent_width, heads_dev, DN)
    q_lat = jnp.einsum("qhn,chn->qhc", query_lo, w_key, preferred_element_type=jnp.float32).astype(
        jnp.bfloat16
    )
    q_lat = q_lat.reshape(per_group, query_rows, heads_dev, latent_width)
    request_ids = jnp.arange(per_group, dtype=jnp.int32)
    token_ids = jnp.arange(block, dtype=jnp.int32)
    start_top = jnp.full((per_group, query_rows, heads_dev), NEG, jnp.float32)
    latent_piece = lax.all_gather(own_latent, DEV, axis=0, tiled=True)
    rope_piece = lax.all_gather(own_rope, DEV, axis=0, tiled=True)
    score = jnp.einsum(
        "pqhc,pkc->pqhk", q_lat[page_req], latent_piece, preferred_element_type=jnp.float32
    )
    score = score + jnp.einsum(
        "pqhr,prk->pqhk", query_hi[page_req], rope_piece, preferred_element_type=jnp.float32
    )
    score = score * scale
    live = token_ids[None, None, None, :] < page_valid[:, None, None, None]
    score = jnp.where(live, score, NEG)
    onehot = page_req[:, None] == request_ids[None, :]
    page_top = jnp.max(score, axis=3)
    piece_top = jnp.max(jnp.where(onehot[:, :, None, None], page_top[:, None], NEG), axis=0)
    top_new = jnp.maximum(start_top, piece_top)
    expo = jnp.where(live, jnp.exp(score - top_new[page_req][..., None]), 0.0)
    select = onehot.astype(jnp.float32)
    total_new = jnp.einsum(
        "pr,pqh->rqh", select, jnp.sum(expo, axis=3), precision=lax.Precision.HIGHEST
    )
    values = jnp.einsum(
        "pqhk,pkc->pqhc",
        expo.astype(jnp.bfloat16),
        latent_piece,
        preferred_element_type=jnp.float32,
    )
    acc_new = jnp.einsum("pr,pqhc->rqhc", select, values, precision=lax.Precision.HIGHEST)
    o_lat = (
        (acc_new / total_new[..., None])
        .astype(jnp.bfloat16)
        .reshape(per_group * query_rows, heads_dev, latent_width)
    )
    w_val = w_uv.reshape(latent_width, heads_dev, DV)
    heads_out = jnp.einsum("qhc,chv->qhv", o_lat, w_val, preferred_element_type=jnp.float32).astype(
        jnp.bfloat16
    )
    heads_out = heads_out.reshape(per_group * query_rows, heads_dev * DV)
    mixed = summed_rows(
        lax.dot_general(
            w_o, heads_out, (((0,), (1,)), ((), ())), preferred_element_type=jnp.float32
        ),
        DEV,
    )
    return mixed.T.astype(jnp.bfloat16)


def solution(mesh):
    split = Mesh(
        mesh.devices.reshape(mesh.shape["grp"], 8, 4, 2), ("grp", "dev_0", "dev_1", "dev_2")
    )
    return jax.shard_map(
        local,
        mesh=split,
        in_specs=(
            P(GRP_DEV, None, None),
            P(GRP_DEV, None, None),
            P(None, DEV),
            P(None, DEV),
            P(None, DEV),
            P(None, DEV),
            P(DEV, None),
            P(),
            P(),
            P(),
            P(),
        ),
        out_specs=P("grp", DEV),
        check_vma=False,
    )
```

profile of v0, /device:TPU:1, one launch (start us, length us, event | category | flops | bytes accessed | tf_op | source)
XLA Modules:
  0.0 423.7 jit_solution(13524470347480903052)
XLA Ops:
  14.5 4.3 %select_select_fusion.2 = s32[256,1]{0,1:T(1,128)S(1)} fusion(s32[]{:T(128)} %bitcast.25, s32[]{:T(128)} %bitcast.26, s32[]{:T(128)} %bitcast.27, s32[]{:T(128)} %bitcast.28, s32[]{:T(128)} %bitcast.29, s32[]{:T(128)} %bitcast.31, s32[]{:T(128)} %bitcast.30), kind=kLoop, calls=%fused_computation.134 | loop fusion | flops 5888 | bytes 1052 | tf_op jit(solution)/shard_map/gather | solution.py:77
  18.8 15.7 %fusion.32 = (s32[256]{0:T(256)S(1)}, s32[256]{0:T(256)S(1)}) fusion(s32[256]{0:T(256)S(1)} %get-tuple-element.31, pred[256]{0:T(512)(128)(4,1)S(1)} %compare_reduce_fusion, pred[256]{0:T(512)(128)(4,1)S(1)} %compare_reduce_fusion.1, pred[256]{0:T(512)(128)(4,1)S(1)} %compare_reduce_fusion.2, pred[256]{0:T(512)(128)(4,1)S(1)} %compare_reduce_fusion.3, ...), kind=kLoop, calls=%fused_computation.129 | loop fusion | flops 9728 | bytes 10596 | tf_op jit(solution)/shard_map/add | solution.py:82
  41.3 4.4 %maximum_bitcast_fusion = bf16[4,1,147456]{2,0,1:T(4,128)(2,1)S(1)} fusion(bf16[4,16384]{1,0:T(4,128)(2,1)S(1)} %broadcast_select_fusion.1, bf16[4,131072]{1,0:T(4,128)(2,1)S(1)} %broadcast_select_fusion), kind=kLoop, calls=%fused_computation.33 | loop fusion | flops 2359296 | bytes 2359296 | tf_op jit(solution)/shard_map/all_to_all | solution.py:21
  50.7 5.0 %all-to-all-start = ((bf16[4,2,73728]{2,1,0:T(2,128)(2,1)}), bf16[4,2,73728]{2,1,0:T(2,128)(2,1)}, u32[]{:S(2)}, u32[]{:S(2)}) async-start(bf16[4,2,73728]{2,1,0:T(2,128)(2,1)} %reshape.904), calls=%async_computation | async-start | bytes 2359296 | tf_op jit(solution)/shard_map/all_to_all | solution.py:21
  57.4 12.5 %all-to-all-done = bf16[4,2,73728]{2,1,0:T(2,128)(2,1)} async-done(((bf16[4,2,73728]{2,1,0:T(2,128)(2,1)}), bf16[4,2,73728]{2,1,0:T(2,128)(2,1)}, u32[]{:S(2)}, u32[]{:S(2)}) %all-to-all-start) | async-done | bytes 1179680 | tf_op jit(solution)/shard_map/all_to_all | solution.py:21
  69.9 2.7 reshape.905
  72.6 2.5 copy.99
  82.9 4.3 %select_select_fusion.1 = s32[256,1]{0,1:T(1,128)S(1)} fusion(s32[]{:T(128)} %bitcast.61, s32[]{:T(128)} %bitcast.62, s32[]{:T(128)} %bitcast.63, s32[]{:T(128)} %bitcast.64, s32[]{:T(128)} %bitcast.65, s32[]{:T(128)} %bitcast.67, s32[]{:T(128)} %bitcast.66), kind=kLoop, calls=%fused_computation.133 | loop fusion | flops 5888 | bytes 1052 | tf_op jit(solution)/shard_map/gather | solution.py:103
  88.0 15.5 %select_select_fusion.3 = s32[256]{0:T(256)S(1)} fusion(pred[256]{0:T(512)(128)(4,1)S(1)} %compare_reduce_fusion, pred[256]{0:T(512)(128)(4,1)S(1)} %compare_reduce_fusion.1, pred[256]{0:T(512)(128)(4,1)S(1)} %compare_reduce_fusion.2, pred[256]{0:T(512)(128)(4,1)S(1)} %compare_reduce_fusion.3, pred[256]{0:T(512)(128)(4,1)S(1)} %compare_reduce_fusion.4, ...), kind=kLoop, calls=%fused_computation.135 | loop fusion | flops 6400 | bytes 8548 | tf_op jit(solution)/shard_map/gather | solution.py:103
  105.2 2.7 gather_fusion.3
  110.1 4.3 %select_select_fusion = s32[256,1]{0,1:T(1,128)S(1)} fusion(s32[]{:T(128)} %bitcast.96, s32[]{:T(128)} %bitcast.97, s32[]{:T(128)} %bitcast.98, s32[]{:T(128)} %bitcast.99, s32[]{:T(128)} %bitcast.100, s32[]{:T(128)} %bitcast.102, s32[]{:T(128)} %bitcast.101), kind=kLoop, calls=%fused_computation.132 | loop fusion | flops 5888 | bytes 1052 | tf_op jit(solution)/shard_map/gather | solution.py:86
  115.2 15.5 %fusion.37 = s32[256]{0:T(256)S(1)} fusion(pred[256]{0:T(512)(128)(4,1)S(1)} %compare_reduce_fusion, pred[256]{0:T(512)(128)(4,1)S(1)} %compare_reduce_fusion.1, pred[256]{0:T(512)(128)(4,1)S(1)} %compare_reduce_fusion.2, pred[256]{0:T(512)(128)(4,1)S(1)} %compare_reduce_fusion.3, pred[256]{0:T(512)(128)(4,1)S(1)} %compare_reduce_fusion.4, ...), kind=kLoop, calls=%fused_computation.139 | loop fusion | flops 8704 | bytes 8548 | tf_op jit(solution)/shard_map/jit(clip)/min | solution.py:86
  132.4 49.0 %all-gather.3.cloned.1.call-done = bf16[64,256,512]{2,1,0:T(8,128)(2,1)} async-done(((bf16[1,256,512]{2,1,0:T(8,128)(2,1)}), bf16[64,256,512]{2,1,0:T(8,128)(2,1)}) %all-gather.3.cloned.1.call-update) | async-done | bytes 16777232 | tf_op jit(solution)/shard_map/all_gather | solution.py:121
  181.4 11.6 %fusion.2 = f32[64,32,2,256]{3,1,2,0:T(8,128)} fusion(bf16[64,32,2,512]{3,1,2,0:T(8,128)(2,1)} %gather_fusion.3, bf16[64,256,512]{2,1,0:T(8,128)(2,1)} %all-gather.3.cloned.1.call-done), kind=kOutput, calls=%fused_computation.17 | convolution fusion | flops 1073741824 | bytes 25165824 | tf_op jit(solution)/shard_map/pqhc,pkc->pqhk/dot_general | solution.py:123
  193.0 65.4 %all-gather.5.cloned.1.call-done = bf16[64,64,256]{2,1,0:T(8,128)(2,1)} async-done(((bf16[1,64,256]{2,1,0:T(8,128)(2,1)}), bf16[64,64,256]{2,1,0:T(8,128)(2,1)}) %all-gather.5.cloned.1.call-update) | async-done | bytes 2097168 | tf_op jit(solution)/shard_map/all_gather | solution.py:122
  258.4 5.7 %fusion.56 = (f32[64,32,2]{1,2,0:T(2,128)S(1)}, f32[64,32,2,256]{3,1,2,0:T(8,128)}) fusion(f32[64,32,2,256]{3,1,2,0:T(8,128)} %fusion.2, bf16[64,32,2,64]{3,1,2,0:T(8,128)(2,1)S(1)} %gather_fusion.7, bf16[64,64,256]{2,1,0:T(8,128)(2,1)} %all-gather.5.cloned.1.call-done, pred[64,256]{1,0:T(8,128)(4,1)S(1)} %iota_compare_fusion.1), kind=kOutput, calls=%fused_computation.171 | convolution fusion | flops 138407936 | bytes 11042816 | tf_op jit(solution)/shard_map/pqhr,prk->pqhk/dot_general | solution.py:126
  265.1 3.2 fusion.6
  268.5 9.6 %fusion = f32[64,32,2,512]{3,1,2,0:T(8,128)S(1)} fusion(bf16[64,256,512]{2,1,0:T(8,128)(2,1)} %all-gather.3.cloned.1.call-done, f32[64,32,2,256]{3,1,2,0:T(8,128)} %get-tuple-element.136, f32[64,32,2]{1,2,0:T(2,128)S(1)} %gather_fusion.8, pred[64,256]{1,0:T(8,128)(4,1)S(1)} %iota_compare_fusion.1), kind=kOutput, calls=%fused_computation.15 | convolution fusion | flops 1076887552 | bytes 29392896 | tf_op jit(solution)/shard_map/pqhk,pkc->pqhc/dot_general | solution.py:141
  278.1 7.5 %fusion.16 = bf16[8,32,2,512]{3,0,2,1:T(8,128)(2,1)S(1)} fusion(f32[64,32,2,512]{3,1,2,0:T(8,128)S(1)} %fusion, f32[8,32,2]{0,2,1:T(2,128)S(1)} %copy.61, s32[64]{0:T(128)S(1)} %get-tuple-element.37), kind=kOutput, calls=%fused_computation.31 | convolution fusion | flops 201851392 | bytes 8915200 | tf_op jit(solution)/shard_map/pr,pqhc->rqhc/dot_general | solution.py:147
  286.3 4.1 convolution_bitcast_fusion
  290.5 82.5 %reduce-scatter.8.cloned.1.call-done = f32[896,256]{0,1:T(8,128)} async-done(((f32[7168,256]{0,1:T(8,128)}), f32[896,256]{0,1:T(8,128)}) %reduce-scatter.8.cloned.1.call-update) | async-done | bytes 917520 | tf_op jit(solution)/shard_map/reduce_scatter | solution.py:30
  372.9 2.4 copy.69
  375.4 22.8 %reduce-scatter.10.cloned.1.call-done = f32[224,256]{1,0:T(8,128)} async-done(((f32[896,256]{1,0:T(8,128)}), f32[224,256]{1,0:T(8,128)}) %reduce-scatter.10.cloned.1.call-update) | async-done | bytes 229392
  398.2 17.2 %reduce-scatter.12.cloned.1.call-done = f32[112,256]{1,0:T(8,128)} async-done(((f32[224,256]{1,0:T(8,128)}), f32[112,256]{1,0:T(8,128)}) %reduce-scatter.12.cloned.1.call-update) | async-done | bytes 114704
  (122 shorter events, 39.3 us)
Async XLA Ops:
  6.5 31.2 %copy-start = (bf16[2,256,512]{2,1,0:T(8,128)(2,1)S(1)}, bf16[2,256,512]{2,1,0:T(8,128)(2,1)}, u32[]{:S(2)}) copy-start(bf16[2,256,512]{2,1,0:T(8,128)(2,1)} %param.11) | copy-start | bytes 1572868
  50.7 19.2 %all-to-all-start = ((bf16[4,2,73728]{2,1,0:T(2,128)(2,1)}), bf16[4,2,73728]{2,1,0:T(2,128)(2,1)}, u32[]{:S(2)}, u32[]{:S(2)}) async-start(bf16[4,2,73728]{2,1,0:T(2,128)(2,1)} %reshape.904), calls=%async_computation | async-start | bytes 2359296 | tf_op jit(solution)/shard_map/all_to_all | solution.py:21
  55.7 125.7 %all-gather.3.cloned.1.call-start = ((), (), s32[]{:S(2)}) async-start(), calls=%async_computation.4 | async-start | bytes 17039360 | tf_op jit(solution)/shard_map/all_gather | solution.py:121
  72.6 7.4 %copy-start.5 = (bf16[1024,256]{1,0:T(8,128)(2,1)S(1)}, bf16[1024,256]{1,0:T(8,128)(2,1)}, u32[]{:S(2)}) copy-start(bf16[1024,256]{1,0:T(8,128)(2,1)} %param.13) | copy-start | bytes 1572868
  75.1 1.0 copy-start.3
  75.1 6.1 %copy-start.6 = (bf16[1024,128]{1,0:T(8,128)(2,1)S(1)}, bf16[1024,128]{1,0:T(8,128)(2,1)}, u32[]{:S(2)}) copy-start(bf16[1024,128]{1,0:T(8,128)(2,1)} %param.14) | copy-start | bytes 786436
  75.2 29.7 %copy-start.7 = (bf16[512,256]{1,0:T(8,128)(2,1)S(1)}, bf16[512,256]{1,0:T(8,128)(2,1)}, u32[]{:S(2)}) copy-start(bf16[512,256]{1,0:T(8,128)(2,1)} %param.15) | copy-start | bytes 786436
  77.5 180.9 %all-gather.5.cloned.1.call-start = ((), (), s32[]{:S(2)}) async-start(), calls=%async_computation.5 | async-start | bytes 2129920 | tf_op jit(solution)/shard_map/all_gather | solution.py:122
  79.1 293.8 %reduce-scatter.8.cloned.1.call-start = ((), (), s32[]{:S(2)}) async-start(), calls=%async_computation.6 | async-start | bytes 8257536 | tf_op jit(solution)/shard_map/reduce_scatter | solution.py:30
  105.2 3.5 copy-start.2
  105.2 26.9 %copy-start.8 = (bf16[512,256]{1,0:T(8,128)(2,1)S(1)}, bf16[512,256]{1,0:T(8,128)(2,1)}, u32[]{:S(2)}) copy-start(bf16[512,256]{1,0:T(8,128)(2,1)} %param.16) | copy-start | bytes 786436
  278.1 8.1 %copy-start.4 = (bf16[256,7168]{1,0:T(8,128)(2,1)S(1)}, bf16[256,7168]{1,0:T(8,128)(2,1)}, u32[]{:S(2)}) copy-start(bf16[256,7168]{1,0:T(8,128)(2,1)} %param.17) | copy-start | bytes 11010052
  290.4 126.8 %copy-start.1 = (bf16[2,256,512]{2,1,0:T(8,128)(2,1)S(1)}, bf16[2,256,512]{2,1,0:T(8,128)(2,1)}, u32[]{:S(2)}) copy-start(bf16[2,256,512]{2,1,0:T(8,128)(2,1)} %param.11) | copy-start | bytes 1572868
  290.4 107.8 %reduce-scatter.10.cloned.1.call-start = ((), (), s32[]{:S(2)}) async-start(), calls=%async_computation.7 | async-start | bytes 1146880
  375.4 40.1 %reduce-scatter.12.cloned.1.call-start = ((), (), s32[]{:S(2)}) async-start(), calls=%async_computation.8 | async-start | bytes 344064
Sparse Core Ops, SparseCore 0:
  77.6 103.7 all-gather.2
  184.1 74.2 all-gather.4
  290.5 82.3 reduce-scatter.7
  375.5 22.6 reduce-scatter.9
  400.6 14.8 reduce-scatter.11
where the time goes:
time: 425 us; the launch traced here: 424 us
  waiting for transfers between devices  249 us (59%)
  other arithmetic  73.1 us (17%)
  local copies, waits for them, and re-layouts  42.8 us (10%)
  matrix products  39.3 us (9%)
  between operations  13.8 us (3%)
  starting transfers between devices  5.18 us (1%)
    reduce_scatter x1, waiting for transfers between devices, summed_rows(): so_far = lax.psum_scatter(so_far, axis, scatter_dimension=0, tiled=True)  82.5 us
    all_gather x1, waiting for transfers between devices, local(): rope_piece = lax.all_gather(own_rope, DEV, axis=0, tiled=True)  65.4 us
    all_gather x1, waiting for transfers between devices, local(): latent_piece = lax.all_gather(own_latent, DEV, axis=0, tiled=True)  49 us
    unnamed x7, waiting for transfers between devices  40.1 us
    gather x2, other arithmetic, local(): page_req = place_values(pos_target, rank[entry_req], group_pages, jnp.int32)  19.8 us
    add x1, other arithmetic, local(): entry_key = entry_col * groups + entry_group  15.7 us
    min x1, other arithmetic, local(): entry_valid = jnp.clip(slot_len[entry_req] - entry_block * block, 0, block)  15.5 us
    unnamed x28, local copies, waits for them, and re-layouts  13.8 us
  transfers between devices with their start and end apart: 6, of which 6 were waited for; matrix products, arithmetic and copies ran while one was open for 16% of the time, Pallas kernels for 0%

commit v1 on v0

--- a/solution.py
+++ b/solution.py
@@ -48,6 +48,15 @@
     preempted,
     assignment,
 ):
+
+    def build_stocks(chunk):
+        return jnp.concatenate(
+            jax.lax.all_to_all(
+                jnp.stack([chunk for _ in range(jax.lax.axis_size(DEV))]), DEV, 0, 0
+            ),
+            axis=0,
+        )
+
     groups = lax.axis_size("grp")
     columns = lax.axis_size(DEV)
     group = lax.axis_index("grp")
@@ -118,7 +127,7 @@
     request_ids = jnp.arange(per_group, dtype=jnp.int32)
     token_ids = jnp.arange(block, dtype=jnp.int32)
     start_top = jnp.full((per_group, query_rows, heads_dev), NEG, jnp.float32)
-    latent_piece = lax.all_gather(own_latent, DEV, axis=0, tiled=True)
+    latent_piece = build_stocks(own_latent)
     rope_piece = lax.all_gather(own_rope, DEV, axis=0, tiled=True)
     score = jnp.einsum(
         "pqhc,pkc->pqhk", q_lat[page_req], latent_piece, preferred_element_type=jnp.float32

time: 425 us -> 652 us (1.53)
  waiting for transfers between devices: 249 us -> 457 us
  starting transfers between devices: 5.18 us -> 20.4 us
    all_to_all x0 -> x1, waiting for transfers between devices: none -> 314 us  [build_stocks(): jax.lax.all_to_all(jnp.stack([chunk for _ in range(jax.lax.axis_size(DEV)...]
    all_gather x1, waiting for transfers between devices: 65.4 us -> 0.01 us  [local(): rope_piece = lax.all_gather(own_rope, DEV, axis=0, tiled=True)]
    all_gather x1 -> x0, waiting for transfers between devices: 49 us -> none  [local(): latent_piece = lax.all_gather(own_latent, DEV, axis=0, tiled=True)]
    all_to_all x0 -> x1, starting transfers between devices: none -> 15.2 us  [build_stocks(): jax.lax.all_to_all(jnp.stack([chunk for _ in range(jax.lax.axis_size(DEV)...]
    reduce_scatter x1, waiting for transfers between devices: 82.5 us -> 90.9 us  [summed_rows(): so_far = lax.psum_scatter(so_far, axis, scatter_dimension=0, tiled=True)]
    unnamed x28 -> x30, local copies, waits for them, and re-layouts: 13.8 us -> 13.8 us
    unnamed x7 -> x6, waiting for transfers between devices: 40.1 us -> 40.1 us
  transfers between devices with their start and end apart: 6 -> 6, of which waited for: 6 -> 5; matrix products, arithmetic and copies ran while one was open for 16% -> 10% of each run, Pallas kernels for 0% -> 0%
where the time goes in v1:
time: 652 us; the launch traced here: 650 us
  waiting for transfers between devices  457 us (70%)
  other arithmetic  72.2 us (11%)
  local copies, waits for them, and re-layouts  47.4 us (7%)
  matrix products  39.2 us (6%)
  starting transfers between devices  20.4 us (3%)
  between operations  13.8 us (2%)
    all_to_all x1, waiting for transfers between devices, build_stocks(): jax.lax.all_to_all(jnp.stack([chunk for _ in range(jax.lax.axis_size(DEV)...  314 us
    reduce_scatter x1, waiting for transfers between devices, summed_rows(): so_far = lax.psum_scatter(so_far, axis, scatter_dimension=0, tiled=True)  90.9 us
    unnamed x6, waiting for transfers between devices  40.1 us
    gather x2, other arithmetic, local(): page_req = place_values(pos_target, rank[entry_req], group_pages, jnp.int32)  19.3 us
    add x1, other arithmetic, local(): entry_key = entry_col * groups + entry_group  15.7 us
    all_to_all x1, starting transfers between devices, build_stocks(): jax.lax.all_to_all(jnp.stack([chunk for _ in range(jax.lax.axis_size(DEV)...  15.2 us
    min x1, other arithmetic, local(): entry_valid = jnp.clip(slot_len[entry_req] - entry_block * block, 0, block)  15.1 us
    unnamed x30, local copies, waits for them, and re-layouts  13.8 us
  transfers between devices with their start and end apart: 6, of which 5 were waited for; matrix products, arithmetic and copies ran while one was open for 10% of the time, Pallas kernels for 0%

profile of v1, /device:TPU:1, one launch (start us, length us, event | category | flops | bytes accessed | tf_op | source)
XLA Modules:
  0.0 650.4 jit_solution(13827955965876753969)
XLA Ops:
  14.5 4.3 select_select_fusion.2
  18.8 15.7 %fusion.32 = (s32[256]{0:T(256)S(1)}, s32[256]{0:T(256)S(1)}) fusion(s32[256]{0:T(256)S(1)} %get-tuple-element.31, pred[256]{0:T(512)(128)(4,1)S(1)} %compare_reduce_fusion, pred[256]{0:T(512)(128)(4,1)S(1)} %compare_reduce_fusion.1, pred[256]{0:T(512)(128)(4,1)S(1)} %compare_reduce_fusion.2, pred[256]{0:T(512)(128)(4,1)S(1)} %compare_reduce_fusion.3, ...), kind=kLoop, calls=%fused_computation.130 | loop fusion | flops 9728 | bytes 10596 | tf_op jit(solution)/shard_map/add | solution.py:91
  40.5 4.4 maximum_bitcast_fusion
  49.9 5.0 all-to-all-start
  56.6 12.5 %all-to-all-done = bf16[4,2,73728]{2,1,0:T(2,128)(2,1)} async-done(((bf16[4,2,73728]{2,1,0:T(2,128)(2,1)}), bf16[4,2,73728]{2,1,0:T(2,128)(2,1)}, u32[]{:S(2)}, u32[]{:S(2)}) %all-to-all-start) | async-done | bytes 1179680 | tf_op jit(solution)/shard_map/all_to_all | solution.py:21
  69.1 2.7 reshape.912
  71.8 2.5 copy.99
  75.9 6.0 stack.2
  81.9 15.2 %all-to-all-start.1 = ((bf16[64,1,256,512]{3,2,1,0:T(8,128)(2,1)}), bf16[64,1,256,512]{3,2,1,0:T(8,128)(2,1)}, u32[]{:S(2)}, u32[]{:S(2)}) async-start(bf16[64,1,256,512]{3,2,1,0:T(8,128)(2,1)} %stack.2), calls=%async_computation.1 | async-start | bytes 33554432 | tf_op jit(solution)/shard_map/all_to_all | solution.py:54
  102.6 4.1 select_select_fusion.1
  107.4 15.2 %select_select_fusion.3 = s32[256]{0:T(256)S(1)} fusion(pred[256]{0:T(512)(128)(4,1)S(1)} %compare_reduce_fusion, pred[256]{0:T(512)(128)(4,1)S(1)} %compare_reduce_fusion.1, pred[256]{0:T(512)(128)(4,1)S(1)} %compare_reduce_fusion.2, pred[256]{0:T(512)(128)(4,1)S(1)} %compare_reduce_fusion.3, pred[256]{0:T(512)(128)(4,1)S(1)} %compare_reduce_fusion.4, ...), kind=kLoop, calls=%fused_computation.136 | loop fusion | flops 6400 | bytes 8548 | tf_op jit(solution)/shard_map/gather | solution.py:112
  124.4 2.9 gather_fusion.3
  129.4 4.3 select_select_fusion
  134.4 15.1 %fusion.37 = s32[256]{0:T(256)S(1)} fusion(pred[256]{0:T(512)(128)(4,1)S(1)} %compare_reduce_fusion, pred[256]{0:T(512)(128)(4,1)S(1)} %compare_reduce_fusion.1, pred[256]{0:T(512)(128)(4,1)S(1)} %compare_reduce_fusion.2, pred[256]{0:T(512)(128)(4,1)S(1)} %compare_reduce_fusion.3, pred[256]{0:T(512)(128)(4,1)S(1)} %compare_reduce_fusion.4, ...), kind=kLoop, calls=%fused_computation.140 | loop fusion | flops 8704 | bytes 8548 | tf_op jit(solution)/shard_map/jit(clip)/min | solution.py:95
  151.2 313.9 %all-to-all-done.1 = bf16[64,1,256,512]{3,2,1,0:T(8,128)(2,1)} async-done(((bf16[64,1,256,512]{3,2,1,0:T(8,128)(2,1)}), bf16[64,1,256,512]{3,2,1,0:T(8,128)(2,1)}, u32[]{:S(2)}, u32[]{:S(2)}) %all-to-all-start.1) | async-done | bytes 16777248 | tf_op jit(solution)/shard_map/all_to_all | solution.py:54
  465.1 11.6 %fusion.2 = f32[64,32,2,256]{3,1,2,0:T(8,128)} fusion(bf16[64,32,2,512]{3,1,2,0:T(8,128)(2,1)} %gather_fusion.3, bf16[64,1,256,512]{3,2,1,0:T(8,128)(2,1)} %all-to-all-done.1), kind=kOutput, calls=%fused_computation.17 | convolution fusion | flops 1073741824 | bytes 25165824 | tf_op jit(solution)/shard_map/pqhc,pkc->pqhk/dot_general | solution.py:132
  476.7 5.7 fusion.56
  483.3 3.2 fusion.6
  486.7 9.6 %fusion = f32[64,32,2,512]{3,1,2,0:T(8,128)S(1)} fusion(bf16[64,1,256,512]{3,2,1,0:T(8,128)(2,1)} %all-to-all-done.1, f32[64,32,2,256]{3,1,2,0:T(8,128)} %get-tuple-element.136, f32[64,32,2]{1,2,0:T(2,128)S(1)} %gather_fusion.8, pred[64,256]{1,0:T(8,128)(4,1)S(1)} %iota_compare_fusion.1), kind=kOutput, calls=%fused_computation.15 | convolution fusion | flops 1076887552 | bytes 29392896 | tf_op jit(solution)/shard_map/pqhk,pkc->pqhc/dot_general | solution.py:150
  496.4 7.5 %fusion.16 = bf16[8,32,2,512]{3,0,2,1:T(8,128)(2,1)S(1)} fusion(f32[64,32,2,512]{3,1,2,0:T(8,128)S(1)} %fusion, f32[8,32,2]{0,2,1:T(2,128)S(1)} %copy.61, s32[64]{0:T(128)S(1)} %get-tuple-element.37), kind=kOutput, calls=%fused_computation.31 | convolution fusion | flops 201851392 | bytes 8915200 | tf_op jit(solution)/shard_map/pr,pqhc->rqhc/dot_general | solution.py:156
  504.5 4.1 convolution_bitcast_fusion
  508.7 90.9 %reduce-scatter.8.cloned.1.call-done = f32[896,256]{0,1:T(8,128)} async-done(((f32[7168,256]{0,1:T(8,128)}), f32[896,256]{0,1:T(8,128)}) %reduce-scatter.8.cloned.1.call-update) | async-done | bytes 917520 | tf_op jit(solution)/shard_map/reduce_scatter | solution.py:30
  602.1 22.7 %reduce-scatter.10.cloned.1.call-done = f32[224,256]{1,0:T(8,128)} async-done(((f32[896,256]{1,0:T(8,128)}), f32[224,256]{1,0:T(8,128)}) %reduce-scatter.10.cloned.1.call-update) | async-done | bytes 229392
  624.7 17.4 %reduce-scatter.12.cloned.1.call-done = f32[112,256]{1,0:T(8,128)} async-done(((f32[224,256]{1,0:T(8,128)}), f32[112,256]{1,0:T(8,128)}) %reduce-scatter.12.cloned.1.call-update) | async-done | bytes 114704
  (124 shorter events, 40.1 us)
Async XLA Ops:
  6.5 29.7 %copy-start = (bf16[2,256,512]{2,1,0:T(8,128)(2,1)S(1)}, bf16[2,256,512]{2,1,0:T(8,128)(2,1)}, u32[]{:S(2)}) copy-start(bf16[2,256,512]{2,1,0:T(8,128)(2,1)} %param.11) | copy-start | bytes 1572868
  6.5 31.2 %copy-start.9 = (bf16[2,64,256]{2,1,0:T(8,128)(2,1)S(1)}, bf16[2,64,256]{2,1,0:T(8,128)(2,1)}, u32[]{:S(2)}) copy-start(bf16[2,64,256]{2,1,0:T(8,128)(2,1)} %param.12) | copy-start | bytes 196612
  49.9 19.2 %all-to-all-start = ((bf16[4,2,73728]{2,1,0:T(2,128)(2,1)}), bf16[4,2,73728]{2,1,0:T(2,128)(2,1)}, u32[]{:S(2)}, u32[]{:S(2)}) async-start(bf16[4,2,73728]{2,1,0:T(2,128)(2,1)} %reshape.911), calls=%async_computation | async-start | bytes 2359296 | tf_op jit(solution)/shard_map/all_to_all | solution.py:21
  74.3 1.0 copy-start.3
  81.9 17.8 %copy-start.5 = (bf16[1024,256]{1,0:T(8,128)(2,1)S(1)}, bf16[1024,256]{1,0:T(8,128)(2,1)}, u32[]{:S(2)}) copy-start(bf16[1024,256]{1,0:T(8,128)(2,1)} %param.13) | copy-start | bytes 1572868
  81.9 19.0 %copy-start.6 = (bf16[1024,128]{1,0:T(8,128)(2,1)S(1)}, bf16[1024,128]{1,0:T(8,128)(2,1)}, u32[]{:S(2)}) copy-start(bf16[1024,128]{1,0:T(8,128)(2,1)} %param.14) | copy-start | bytes 786436
  81.9 42.2 %copy-start.7 = (bf16[512,256]{1,0:T(8,128)(2,1)S(1)}, bf16[512,256]{1,0:T(8,128)(2,1)}, u32[]{:S(2)}) copy-start(bf16[512,256]{1,0:T(8,128)(2,1)} %param.15) | copy-start | bytes 786436
  81.9 383.2 %all-to-all-start.1 = ((bf16[64,1,256,512]{3,2,1,0:T(8,128)(2,1)}), bf16[64,1,256,512]{3,2,1,0:T(8,128)(2,1)}, u32[]{:S(2)}, u32[]{:S(2)}) async-start(bf16[64,1,256,512]{3,2,1,0:T(8,128)(2,1)} %stack.2), calls=%async_computation.1 | async-start | bytes 33554432 | tf_op jit(solution)/shard_map/all_to_all | solution.py:54
  97.1 379.6 %all-gather.2.cloned.1.call-start = ((), (), s32[]{:S(2)}) async-start(), calls=%async_computation.5 | async-start | bytes 2129920 | tf_op jit(solution)/shard_map/all_gather | solution.py:131
  98.8 500.8 %reduce-scatter.8.cloned.1.call-start = ((), (), s32[]{:S(2)}) async-start(), calls=%async_computation.6 | async-start | bytes 8257536 | tf_op jit(solution)/shard_map/reduce_scatter | solution.py:30
  124.4 3.6 copy-start.2
  124.4 26.6 %copy-start.8 = (bf16[512,256]{1,0:T(8,128)(2,1)S(1)}, bf16[512,256]{1,0:T(8,128)(2,1)}, u32[]{:S(2)}) copy-start(bf16[512,256]{1,0:T(8,128)(2,1)} %param.16) | copy-start | bytes 786436
  496.3 8.1 %copy-start.4 = (bf16[256,7168]{1,0:T(8,128)(2,1)S(1)}, bf16[256,7168]{1,0:T(8,128)(2,1)}, u32[]{:S(2)}) copy-start(bf16[256,7168]{1,0:T(8,128)(2,1)} %param.17) | copy-start | bytes 11010052
  508.6 135.3 %copy-start.1 = (bf16[2,256,512]{2,1,0:T(8,128)(2,1)S(1)}, bf16[2,256,512]{2,1,0:T(8,128)(2,1)}, u32[]{:S(2)}) copy-start(bf16[2,256,512]{2,1,0:T(8,128)(2,1)} %param.11) | copy-start | bytes 1572868
  508.6 116.1 %reduce-scatter.10.cloned.1.call-start = ((), (), s32[]{:S(2)}) async-start(), calls=%async_computation.7 | async-start | bytes 1146880
  602.0 40.1 %reduce-scatter.12.cloned.1.call-start = ((), (), s32[]{:S(2)}) async-start(), calls=%async_computation.8 | async-start | bytes 344064
Sparse Core Ops, SparseCore 0:
  100.7 136.1 all-gather.1
  508.7 90.7 reduce-scatter.7
  602.1 22.5 reduce-scatter.9
  627.1 15.0 reduce-scatter.11
